TPU v7x, 32 devices: a whole 2x2x4 slice. The times are simulated.
32 devices in a mesh: cls: 4 (over y, x), row: 8 (over z, core).
Axes of the slice: x: 2, y: 2, z: 4, core: 2. Of those that a mesh axis runs over, the one named last changes fastest.
Arguments:
- binned: int32 [32768, 512], P('row'), may hold values from 0 to 255
- labels: int32 [32768], P('row'), may hold values from 0 to 127
- logits: float32 [32768, 128], P('row', 'cls'), may hold values from -320 to 320
- elected: int32 [128, 12], P('cls'), may hold values from 0 to 511, as said below
- split_slot: int32 [128], P('cls'), may hold values from 0 to 11
- split_bin: int32 [128], P('cls'), may hold values from 0 to 254
Outputs:
- new_logits: float32 [32768, 128], P('row', 'cls')
- split_gains: float32 [128, 12, 256], P(('cls', 'row'))
Inputs may be any that keep to these rules, and one draw needn't show every extreme that they name: `elected`: the 12 ids of one class are distinct.
All inputs are finite; a program needn't handle non-finite values.
Results may differ from a plain program's by a relative error of at most 0.002.
Values sent between devices are 32-bit elements; how exact they have to be, the bound alone decides.
A program may use at most 128 MiB of HBM per device.

v0:
```python
import functools
import math

import jax
import jax.numpy as jnp
from jax import lax
from jax.experimental import pallas as pl
from jax.experimental.pallas import tpu as pltpu
from jax.experimental.layout import Layout, with_layout_constraint
from jax.sharding import PartitionSpec as P

reg_lambda = 1.0
step_rate = 0.5
MESH = pl.DeviceIdType.MESH
NT = (((1,), (1,)), ((), ()))
LOW = 32
HIGH = 8
BINS = LOW * HIGH
UNROLL = 2
CHUNK = 1024
BLOCK = 512


def kernel(
    n_cls, n_row, group, groups_each, chunk, unroll,
    binned_ref, x_ref, labels_ref, elected_ref, slot_ref, split_ref,
    new_ref, gains_ref,
    meta, picker, low, high, left, weights, grad_ref, hess_ref, stats, sums,
    theirs, mine, first, second,
    send_stat, recv_stat, send_sum, recv_sum, send_one, recv_one, send_two, recv_two,
):
    step = pl.program_id(0)
    last = pl.num_programs(0) - 1
    block = binned_ref.shape[0]
    classes, rows = x_ref.shape
    features = elected_ref.shape[0]
    pairs = classes * features
    cls = lax.axis_index("cls")
    me = lax.axis_index("row")
    core = lax.rem(me, 2)
    chip = me // 2
    chips = n_row // 2
    barrier = pltpu.get_barrier_semaphore()

    def stat_copy(k):
        return pltpu.make_async_remote_copy(
            src_ref=stats.at[0], dst_ref=stats.at[k], send_sem=send_stat.at[k], recv_sem=recv_stat.at[k],
            device_id=(lax.rem(cls + k, n_cls), me), device_id_type=MESH,
        )

    def sum_copy(k):
        return pltpu.make_async_remote_copy(
            src_ref=sums.at[0], dst_ref=sums.at[k], send_sem=send_sum.at[k], recv_sem=recv_sum.at[k],
            device_id=(cls, lax.rem(me + k, n_row)), device_id_type=MESH,
        )

    def one_copy(s):
        return pltpu.make_async_remote_copy(
            src_ref=theirs.at[s], dst_ref=first.at[s], send_sem=send_one.at[s], recv_sem=recv_one.at[s],
            device_id=(cls, 2 * chip + 1 - core), device_id_type=MESH,
        )

    def two_copy(s):
        return pltpu.make_async_remote_copy(
            src_ref=mine.at[s], dst_ref=second.at[s], send_sem=send_two.at[s], recv_sem=recv_two.at[s],
            device_id=(cls, 2 * lax.rem(chip + s + 1, chips) + core), device_id_type=MESH,
        )

    @pl.when(step == 0)
    def _():
        for k in range(1, n_cls):
            pl.semaphore_signal(
                barrier, inc=1, device_id=(lax.rem(cls + k, n_cls), me), device_id_type=MESH
            )
        for k in range(1, n_row):
            pl.semaphore_signal(
                barrier, inc=1, device_id=(cls, lax.rem(me + k, n_row)), device_id_type=MESH
            )
        x = x_ref[...]
        local_max = jnp.max(x, axis=0, keepdims=True)
        stats[0, 0:1, :] = local_max
        stats[0, 1:2, :] = jnp.sum(jnp.exp(x - local_max), axis=0, keepdims=True)
        meta[...] = jnp.zeros(meta.shape, jnp.float32)
        meta[:features, :classes] = elected_ref[...].astype(jnp.float32)
        meta[features : features + 1, :classes] = slot_ref[...].astype(jnp.float32)
        meta[features + 1 : features + 2, :classes] = split_ref[...].astype(jnp.float32)
        turned = meta[...].T
        meta[...] = turned
        lane = lax.broadcasted_iota(jnp.int32, (classes, picker.shape[1]), 1).astype(jnp.float32)
        slot = turned[:classes, features : features + 1]
        split_feature = jnp.zeros((classes, 1), jnp.float32)
        for k in range(features):
            column = turned[:classes, k : k + 1]
            split_feature = jnp.where(slot == k, column, split_feature)
            picker[k * classes : (k + 1) * classes] = (lane == column).astype(jnp.float32).astype(
                jnp.bfloat16
            )
        picker[pairs:] = (lane == split_feature).astype(jnp.float32).astype(jnp.bfloat16)
        pl.semaphore_wait(barrier, n_cls - 1 + n_row - 1)
        for k in range(1, n_cls):
            stat_copy(k).start()

    here = binned_ref[...].astype(jnp.float32).astype(jnp.bfloat16)
    picked = lax.dot_general(picker[...], here, NT, preferred_element_type=jnp.float32)
    where = pl.ds(pl.multiple_of(step * block, block), block)
    chosen = picked[:pairs].astype(jnp.int32)
    low[:, where] = (chosen & (LOW - 1)).astype(jnp.float32)
    high[:, where] = (chosen >> 5).astype(jnp.float32)
    split_column = meta[:classes, features + 1 : features + 2]
    left[:, where] = (picked[pairs:] <= split_column).astype(jnp.float32)

    @pl.when(step == last)
    def _():
        for k in range(1, n_cls):
            stat_copy(k).wait()
        local_max = stats[0, 0:1, :]
        highest = local_max
        for k in range(1, n_cls):
            highest = jnp.maximum(highest, stats[k, 0:1, :])
        denom = stats[0, 1:2, :] * jnp.exp(local_max - highest)
        for k in range(1, n_cls):
            denom = denom + stats[k, 1:2, :] * jnp.exp(stats[k, 0:1, :] - highest)
        probs = jnp.exp(x_ref[...] - highest) / denom
        class_ids = cls * classes + lax.broadcasted_iota(jnp.int32, probs.shape, 0)
        target = (labels_ref[...] == class_ids).astype(jnp.float32)
        grad = (probs - target).astype(jnp.bfloat16).astype(jnp.float32)
        hess = (probs * (1.0 - probs)).astype(jnp.bfloat16).astype(jnp.float32)
        grad_ref[...] = grad
        hess_ref[...] = hess
        goes = left[...]
        lane = lax.broadcasted_iota(jnp.int32, (classes, 128), 1)
        total = jnp.where(lane == 0, jnp.sum(grad * goes, axis=1, keepdims=True), 0.0)
        total = jnp.where(lane == 1, jnp.sum(hess * goes, axis=1, keepdims=True), total)
        total = jnp.where(lane == 2, jnp.sum(grad, axis=1, keepdims=True), total)
        total = jnp.where(lane == 3, jnp.sum(hess, axis=1, keepdims=True), total)
        sums[0] = total
        for k in range(1, n_row):
            sum_copy(k).start()

        is_grad = lax.broadcasted_iota(jnp.int32, (2 * HIGH, rows), 0) < HIGH

        def expand(c, carry):
            mixed = jnp.where(is_grad, grad_ref[pl.ds(c, 1), :], hess_ref[pl.ds(c, 1), :])
            weights[pl.ds(pl.multiple_of(c * 2 * HIGH, 2 * HIGH), 2 * HIGH), :] = mixed.astype(
                jnp.bfloat16
            )
            return carry

        lax.fori_loop(0, classes, expand, 0)

        sub = lax.broadcasted_iota(jnp.int32, (16, chunk), 0)
        low_first = sub.astype(jnp.float32).astype(jnp.bfloat16)
        low_second = (sub + 16).astype(jnp.float32).astype(jnp.bfloat16)
        high_ids = (sub & (HIGH - 1)).astype(jnp.float32).astype(jnp.bfloat16)
        one = jnp.ones((16, chunk), jnp.bfloat16)
        zero = jnp.zeros((16, chunk), jnp.bfloat16)
        lane_pair = lax.broadcasted_iota(jnp.int32, (2 * HIGH, group * LOW), 1) // LOW

        def one_group(g):
            total = None
            for part in range(rows // chunk):
                cols = pl.ds(part * chunk, chunk)
                lows = []
                highs = []
                for j in range(group):
                    q = g * group + j
                    c = q // features
                    p = (q - c * features) * classes + c
                    lo = jnp.broadcast_to(low[pl.ds(p, 1), cols], (16, chunk)).astype(jnp.bfloat16)
                    hi = jnp.broadcast_to(high[pl.ds(p, 1), cols], (16, chunk)).astype(jnp.bfloat16)
                    w = weights[pl.ds(pl.multiple_of(c * 16, 16), 16), cols]
                    lows.append(jnp.where(lo == low_first, one, zero))
                    lows.append(jnp.where(lo == low_second, one, zero))
                    highs.append(jnp.where(hi == high_ids, w, zero))
                product = lax.dot_general(
                    jnp.concatenate(highs, axis=0), jnp.concatenate(lows, axis=0), NT,
                    preferred_element_type=jnp.float32,
                )
                total = product if total is None else total + product
            kept = total[:16]
            for j in range(1, group):
                kept = jnp.where(lane_pair == j, total[16 * j : 16 * j + 16], kept)
            return kept

        def fill(target_ref, s, dest):
            def some(i, carry):
                for u in range(unroll):
                    target_ref[s, i * unroll + u] = one_group(dest * groups_each + i * unroll + u)
                return carry

            lax.fori_loop(0, groups_each // unroll, some, 0)

        def pass_on(s):
            one_copy(s).wait_recv()
            mine[s] = mine[s] + first[s]
            two_copy(s).start()

        def each_chip(s, carry):
            dest = lax.rem(chip + s + 1, chips)
            fill(theirs, s, 2 * dest + 1 - core)
            one_copy(s).start()
            fill(mine, s, 2 * dest + core)

            @pl.when(s < chips - 1)
            def _():
                pass_on(s)

            return carry

        lax.fori_loop(0, chips, each_chip, 0)

        total = sums[0]
        for k in range(1, n_row):
            sum_copy(k).wait()
            total = total + sums[k]
        grad_left = total[:, 0:1]
        hess_left = total[:, 1:2]
        left_leaf = -grad_left / (hess_left + reg_lambda)
        right_leaf = -(total[:, 2:3] - grad_left) / (total[:, 3:4] - hess_left + reg_lambda)
        new_ref[...] = x_ref[...] + step_rate * jnp.where(left[...] > 0.5, left_leaf, right_leaf)

        one_copy(chips - 1).wait_recv()
        summed = mine[chips - 1] + first[chips - 1]
        for s in range(chips):
            one_copy(s).wait_send()
        for s in range(chips - 1):
            two_copy(s).wait()
            summed = summed + second[s]
        wide = group * LOW
        here = summed.reshape(groups_each * 2 * HIGH, wide)
        a = lax.broadcasted_iota(jnp.int32, (wide, wide), 0)
        b = lax.broadcasted_iota(jnp.int32, (wide, wide), 1)
        same = (a // LOW) == (b // LOW)
        upto = (same & (a <= b)).astype(jnp.float32)
        every = same.astype(jnp.float32)
        inside = jnp.dot(here, upto, precision=lax.Precision.HIGHEST, preferred_element_type=jnp.float32)
        whole = jnp.dot(here, every, precision=lax.Precision.HIGHEST, preferred_element_type=jnp.float32)
        count = groups_each * 2 * HIGH
        r = lax.broadcasted_iota(jnp.int32, (count, count), 0)
        s = lax.broadcasted_iota(jnp.int32, (count, count), 1)
        same_high = (r // HIGH) == (s // HIGH)
        before = jnp.dot((same_high & (s < r)).astype(jnp.float32), whole,
                         precision=lax.Precision.HIGHEST, preferred_element_type=jnp.float32)
        ends = jnp.dot(same_high.astype(jnp.float32), whole,
                       precision=lax.Precision.HIGHEST, preferred_element_type=jnp.float32)
        running = inside + before
        for g in range(groups_each):
            top = g * 2 * HIGH
            gl = running[top : top + HIGH]
            hl = running[top + HIGH : top + 2 * HIGH]
            ga = ends[top : top + HIGH]
            ha = ends[top + HIGH : top + 2 * HIGH]
            gains_ref[g] = (
                gl * gl / (hl + reg_lambda)
                + (ga - gl) * (ga - gl) / (ha - hl + reg_lambda)
                - ga * ga / (ha + reg_lambda)
            )


def local(n_cls, n_row, binned, labels, logits, elected, split_slot, split_bin):
    rows, classes = logits.shape
    columns = binned.shape[1]
    features = elected.shape[1]
    pairs = classes * features
    share = classes // n_row
    group = math.gcd(share * features, 8)
    groups_each = share * features // group
    block = math.gcd(rows, BLOCK)
    chunk = math.gcd(rows, CHUNK)
    unroll = math.gcd(groups_each, UNROLL)
    chips = n_row // 2
    f32 = jnp.float32
    dma = pltpu.SemaphoreType.DMA
    part = (chips, groups_each, 2 * HIGH, group * LOW)

    def whole(*shape):
        return pl.BlockSpec(shape, lambda i: (0,) * len(shape))

    new, gains = pl.pallas_call(
        functools.partial(kernel, n_cls, n_row, group, groups_each, chunk, unroll),
        grid=(rows // block,),
        out_shape=[
            jax.ShapeDtypeStruct((classes, rows), f32),
            jax.ShapeDtypeStruct((groups_each, HIGH, group * LOW), f32),
        ],
        in_specs=[
            pl.BlockSpec((block, columns), lambda i: (i, 0)),
            whole(classes, rows),
            whole(1, rows),
            whole(features, classes),
            whole(1, classes),
            whole(1, classes),
        ],
        out_specs=[whole(classes, rows), whole(groups_each, HIGH, group * LOW)],
        scratch_shapes=[
            pltpu.VMEM((128, 128), f32),
            pltpu.VMEM((pairs + classes, columns), jnp.bfloat16),
            pltpu.VMEM((pairs, rows), f32),
            pltpu.VMEM((pairs, rows), f32),
            pltpu.VMEM((classes, rows), f32),
            pltpu.VMEM((classes * 2 * HIGH, rows), jnp.bfloat16),
            pltpu.VMEM((classes, rows), f32),
            pltpu.VMEM((classes, rows), f32),
            pltpu.VMEM((n_cls, 2, rows), f32),
            pltpu.VMEM((n_row, classes, 128), f32),
            pltpu.VMEM(part, f32), pltpu.VMEM(part, f32), pltpu.VMEM(part, f32), pltpu.VMEM(part, f32),
            dma((n_cls,)), dma((n_cls,)), dma((n_row,)), dma((n_row,)),
            dma((chips,)), dma((chips,)), dma((chips,)), dma((chips,)),
        ],
        compiler_params=pltpu.CompilerParams(
            dimension_semantics=("arbitrary",), vmem_limit_bytes=56 * 1024 * 1024,
            collective_id=0, has_side_effects=True,
        ),
        name="round",
    )(
        binned, logits.T, labels.reshape(1, rows), elected.T,
        split_slot.reshape(1, classes), split_bin.reshape(1, classes),
    )
    gains = gains.reshape(groups_each, HIGH, group, LOW).transpose(0, 2, 1, 3)
    new = with_layout_constraint(new.T, Layout((1, 0)))
    return new, gains.reshape(share, features, BINS)


def solution(mesh):
    return jax.shard_map(
        functools.partial(local, mesh.shape["cls"], mesh.shape["row"]),
        mesh=mesh,
        in_specs=(P("row", None), P("row"), P("row", "cls"), P("cls", None), P("cls"), P("cls")),
        out_specs=(P("row", "cls"), P(("cls", "row"), None, None)),
        check_vma=False,
    )
```

profile of v0, /device:TPU:0, one launch (start us, length us, event | category | flops | bytes accessed | tf_op | source)
XLA Modules:
  0.0 59.5 jit_solution(7143566063394277033)
XLA Ops:
  0.6 55.2 %round.1 = (f32[32,4096]{1,0:T(8,128)}, f32[6,8,256]{2,1,0:T(8,128)}) custom-call(s32[4096,512]{1,0:T(8,128)} %binned_ref.1, f32[32,4096]{1,0:T(8,128)} %bitcast.13, s32[1,4096]{1,0:T(1,128)} %bitcast.14, s32[12,32]{1,0:T(8,128)} %bitcast.15, s32[1,32]{1,0:T(1,128)} %bitcast.16, s32[1,32]{1,0:T(1,128)} %bitcast.17), custom_call_target="tpu_custom_call" | custom-call | tf_op jit(solution)/shard_map/round/pallas_call | solution.py:279
  55.9 0.9 %reshape.22 = f32[6,8,8,32]{3,2,1,0:T(8,128)S(1)} reshape(f32[6,8,256]{2,1,0:T(8,128)} %get-tuple-element.5) | data formatting | bytes 98304 | tf_op jit(solution)/shard_map/reshape | solution.py:319
  56.8 0.1 reshape.23
  56.9 0.7 %copy.9 = f32[4,12,256]{2,0,1:T(4,128)} copy(f32[4,12,256]{2,1,0:T(8,128)S(1)} %reshape.23) | data formatting | bytes 98304
  57.6 1.9 %copy.13 = f32[4096,32]{0,1:T(8,128)} copy(f32[4096,32]{0,1:T(8,128)} %bitcast.12) | data formatting | bytes 1048576
  (1 shorter events, 0.0 us)
where the time goes:
time: 59.8 us; the launch traced here: 59.5 us
  Pallas kernels  55.2 us (92%)
  local copies, waits for them, and re-layouts  3.57 us (6%)
  between operations  0.66 us (1%)
    pallas_call x1, Pallas kernels, local(): pl.pallas_call(functools.partial(kernel, n_cls, n_row, group, groups_each...  55.2 us
    unnamed x2, local copies, waits for them, and re-layouts  2.52 us

commit v1 on v0

v1 whole, which is shorter than its diff:
```python
import functools
import math

import jax
import jax.numpy as jnp
from jax import lax
from jax.experimental import pallas as pl
from jax.experimental.pallas import tpu as pltpu
from jax.sharding import PartitionSpec as P

reg_lambda = 1.0
step_rate = 0.5
MESH = pl.DeviceIdType.MESH
NT = (((1,), (1,)), ((), ()))
LOW = 32
HIGH = 8
BINS = LOW * HIGH
UNROLL = 6
BLOCK = 512
LANES = 128
DEPTH = 256
bf16 = jnp.bfloat16
f32 = jnp.float32
narrow = jnp.float8_e4m3fn


def kernel(
    n_cls, n_row, duos, groups_each, unroll, share,
    binned_hbm, x_hbm, labels_hbm, elected_hbm, slot_hbm, split_hbm,
    new_ref, gains_ref,
    binned_ref, x_ref, labels_ref, elected_ref, slot_ref, split_ref,
    meta, picker, low, high, left, grad_ref, hess_ref, grad_rows, hess_rows, stats, sums,
    theirs, mine, first, second,
    load_sem, send_stat, recv_stat, send_sum, recv_sum, send_one, recv_one, send_two, recv_two,
):
    classes, rows = x_ref.shape
    features = elected_ref.shape[0]
    pairs = classes * features
    block = math.gcd(rows, BLOCK)
    blocks = rows // block
    tiles = rows // LANES
    per_block = block // LANES
    cls = lax.axis_index("cls")
    me = lax.axis_index("row")
    core = lax.rem(me, 2)
    chip = me // 2
    chips = n_row // 2
    barrier = pltpu.get_barrier_semaphore()

    def stat_copy(k):
        return pltpu.make_async_remote_copy(
            src_ref=stats.at[0], dst_ref=stats.at[k], send_sem=send_stat.at[k], recv_sem=recv_stat.at[k],
            device_id=(lax.rem(cls + k, n_cls), me), device_id_type=MESH,
        )

    def sum_copy(k):
        return pltpu.make_async_remote_copy(
            src_ref=sums.at[0], dst_ref=sums.at[k], send_sem=send_sum.at[k], recv_sem=recv_sum.at[k],
            device_id=(cls, lax.rem(me + k, n_row)), device_id_type=MESH,
        )

    def one_copy(s):
        return pltpu.make_async_remote_copy(
            src_ref=theirs.at[s], dst_ref=first.at[s], send_sem=send_one.at[s], recv_sem=recv_one.at[s],
            device_id=(cls, 2 * chip + 1 - core), device_id_type=MESH,
        )

    def two_copy(s):
        return pltpu.make_async_remote_copy(
            src_ref=mine.at[s], dst_ref=second.at[s], send_sem=send_two.at[s], recv_sem=recv_two.at[s],
            device_id=(cls, 2 * lax.rem(chip + s + 1, chips) + core), device_id_type=MESH,
        )

    small = [
        pltpu.make_async_copy(src, dst, load_sem.at[blocks + i])
        for i, (src, dst) in enumerate([
            (elected_hbm, elected_ref), (slot_hbm, slot_ref), (split_hbm, split_ref),
            (x_hbm, x_ref), (labels_hbm, labels_ref),
        ])
    ]
    part = [
        pltpu.make_async_copy(
            binned_hbm.at[pl.ds(b * block, block)], binned_ref.at[pl.ds(b * block, block)], load_sem.at[b]
        )
        for b in range(blocks)
    ]

    for k in range(1, n_cls):
        pl.semaphore_signal(barrier, inc=1, device_id=(lax.rem(cls + k, n_cls), me), device_id_type=MESH)
    for k in range(1, n_row):
        pl.semaphore_signal(barrier, inc=1, device_id=(cls, lax.rem(me + k, n_row)), device_id_type=MESH)
    for copy in small[:4]:
        copy.start()
    for copy in part:
        copy.start()
    small[4].start()

    for copy in small[:3]:
        copy.wait()
    meta[...] = jnp.zeros(meta.shape, f32)
    meta[:features, :classes] = elected_ref[...].astype(f32)
    meta[features : features + 1, :classes] = slot_ref[...].astype(f32)
    meta[features + 1 : features + 2, :classes] = split_ref[...].astype(f32)
    turned = meta[...].T
    lane = lax.broadcasted_iota(jnp.int32, (classes, picker.shape[1]), 1).astype(f32)
    slot = turned[:classes, features : features + 1]
    split_column = turned[:classes, features + 1 : features + 2]
    split_feature = jnp.zeros((classes, 1), f32)
    for k in range(features):
        column = turned[:classes, k : k + 1]
        split_feature = jnp.where(slot == k, column, split_feature)
        picker[k * classes : (k + 1) * classes] = (lane == column).astype(f32).astype(bf16)
    picker[pairs:] = (lane == split_feature).astype(f32).astype(bf16)

    small[3].wait()
    for b in range(blocks):
        cols = slice(b * block, (b + 1) * block)
        x = x_ref[:, cols]
        local_max = jnp.max(x, axis=0, keepdims=True)
        stats[0, 0:1, cols] = local_max
        stats[0, 1:2, cols] = jnp.sum(jnp.exp(x - local_max), axis=0, keepdims=True)

    def pick(b):
        part[b].wait()
        here = binned_ref[b * block : (b + 1) * block].astype(f32).astype(bf16)
        picked = lax.dot_general(picker[...], here, NT, preferred_element_type=f32)
        chosen = picked[:pairs]
        top = jnp.floor(chosen * (1.0 / LOW))
        rest = chosen - top * LOW
        for j in range(per_block):
            low[b * per_block + j] = rest[:, j * LANES : (j + 1) * LANES]
            high[b * per_block + j] = top[:, j * LANES : (j + 1) * LANES]
        left[:, b * block : (b + 1) * block] = (picked[pairs:] <= split_column).astype(f32)

    for b in range(blocks // 2):
        pick(b)
    with jax.named_scope("barrier"):
        pl.semaphore_wait(barrier, n_cls - 1 + n_row - 1)
    for k in range(1, n_cls):
        stat_copy(k).start()
    for b in range(blocks // 2, blocks):
        pick(b)

    small[4].wait()
    with jax.named_scope("statwait"):
        for k in range(1, n_cls):
            stat_copy(k).wait()
    class_ids = cls * classes + lax.broadcasted_iota(jnp.int32, (classes, block), 0)
    totals = [jnp.zeros((classes, LANES), f32) for _ in range(4)]
    for b in range(blocks):
        cols = slice(b * block, (b + 1) * block)
        local_max = stats[0, 0:1, cols]
        highest = local_max
        for k in range(1, n_cls):
            highest = jnp.maximum(highest, stats[k, 0:1, cols])
        denom = stats[0, 1:2, cols] * jnp.exp(local_max - highest)
        for k in range(1, n_cls):
            denom = denom + stats[k, 1:2, cols] * jnp.exp(stats[k, 0:1, cols] - highest)
        probs = jnp.exp(x_ref[:, cols] - highest) / denom
        target = (labels_ref[:, cols] == class_ids).astype(f32)
        grad = (probs - target).astype(bf16).astype(f32)
        hess = (probs * (1.0 - probs)).astype(bf16).astype(f32)
        goes = left[:, cols]
        for j in range(per_block):
            at = slice(j * LANES, (j + 1) * LANES)
            grad_ref[b * per_block + j] = grad[:, at]
            hess_ref[b * per_block + j] = hess[:, at]
            for n, term in enumerate((grad * goes, hess * goes, grad, hess)):
                totals[n] = totals[n] + term[:, at]
    spot = lax.broadcasted_iota(jnp.int32, (classes, LANES), 1)
    packed = jnp.zeros((classes, LANES), f32)
    for n in range(4):
        packed = jnp.where(spot == n, jnp.sum(totals[n], axis=1, keepdims=True), packed)
    sums[0] = packed
    for k in range(1, n_row):
        sum_copy(k).start()

    def repeat(c, carry):
        for t in range(tiles):
            g = grad_ref[t, pl.ds(c, 8, stride=0), :]
            h = hess_ref[t, pl.ds(c, 8, stride=0), :]
            grad_rows[c, t] = jnp.concatenate([g, g], axis=0).astype(bf16)
            hess_rows[c, t] = jnp.concatenate([h, h], axis=0).astype(bf16)
        return carry

    with jax.named_scope("repeat"):
        lax.fori_loop(0, classes, repeat, 0)

    sub = lax.broadcasted_iota(jnp.int32, (16, LANES), 0) & (HIGH - 1)
    ids = [(sub + HIGH * n).astype(f32).astype(bf16) for n in range(LOW // HIGH)]
    one = jnp.ones((16, LANES), bf16)
    zero = jnp.zeros((16, LANES), bf16)
    wide = duos * 2 * LOW
    lane_at = lax.broadcasted_iota(jnp.int32, (16, wide), 1)
    lane_pair = lane_at // (2 * LOW) * 2 + lane_at // HIGH % 2
    depth = math.gcd(rows, DEPTH)

    def one_group(dest, g):
        total = None
        for step in range(rows // depth):
            tops = []
            lows = []
            for d in range(duos):
                q = g * duos + d
                c = dest * share + q % share
                p = q // share * 2 * classes + c
                top = [[], []]
                low_rows = [[] for _ in range(LOW // 16)]
                for t in range(step * depth // LANES, (step + 1) * depth // LANES):

                    def both(ref):
                        a = ref[t, pl.ds(p, 8, stride=0), :]
                        b = ref[t, pl.ds(p + classes, 8, stride=0), :]
                        return jnp.concatenate([a, b], axis=0).astype(bf16)

                    lo = both(low)
                    hot = [jnp.where(lo == i, one, zero) for i in ids]
                    for n in range(LOW // 16):
                        low_rows[n].append(jnp.concatenate(hot[2 * n : 2 * n + 2], axis=0).astype(narrow))
                    same = both(high) == ids[0]
                    top[0].append(jnp.where(same, grad_rows[c, t], zero))
                    top[1].append(jnp.where(same, hess_rows[c, t], zero))
                tops += [jnp.concatenate(r, axis=1) for r in top]
                lows += [jnp.concatenate(r, axis=1) for r in low_rows]
            product = lax.dot_general(
                jnp.concatenate(tops, axis=0), jnp.concatenate(lows, axis=0), NT, preferred_element_type=f32
            )
            total = product if total is None else total + product
        kept = None
        for d in range(duos):
            for s in range(2):
                at = d * 32 + s * 8
                piece = jnp.concatenate([total[at : at + 8], total[at + 16 : at + 24]], axis=0)
                kept = piece if kept is None else jnp.where(lane_pair == 2 * d + s, piece, kept)
        return kept

    def fill(target_ref, s, dest):
        def some(i, carry):
            for u in range(unroll):
                target_ref[s, i * unroll + u] = one_group(dest, i * unroll + u)
            return carry

        lax.fori_loop(0, groups_each // unroll, some, 0)

    def each_chip(s, carry):
        dest = lax.rem(chip + s + 1, chips)
        fill(theirs, s, 2 * dest + 1 - core)
        one_copy(s).start()
        fill(mine, s, 2 * dest + core)

        @pl.when(s < chips - 1)
        def _():
            with jax.named_scope("onewait"):
                one_copy(s).wait_recv()
            mine[s] = mine[s] + first[s]
            two_copy(s).start()

        return carry

    with jax.named_scope("hist"):
        lax.fori_loop(0, chips, each_chip, 0)

    total = sums[0]
    with jax.named_scope("sumwait"):
        for k in range(1, n_row):
            sum_copy(k).wait()
    for k in range(1, n_row):
        total = total + sums[k]
    grad_left = total[:, 0:1]
    hess_left = total[:, 1:2]
    left_leaf = -grad_left / (hess_left + reg_lambda)
    right_leaf = -(total[:, 2:3] - grad_left) / (total[:, 3:4] - hess_left + reg_lambda)
    for b in range(blocks):
        cols = slice(b * block, (b + 1) * block)
        new_ref[:, cols] = x_ref[:, cols] + step_rate * jnp.where(left[:, cols] > 0.5, left_leaf, right_leaf)

    with jax.named_scope("tailwait"):
        one_copy(chips - 1).wait_recv()
        for s in range(chips):
            one_copy(s).wait_send()
        for s in range(chips - 1):
            two_copy(s).wait()
    summed = mine[chips - 1] + first[chips - 1]
    for s in range(chips - 1):
        summed = summed + second[s]
    count = groups_each * 2 * HIGH
    here = summed.reshape(count, wide)
    a = lax.broadcasted_iota(jnp.int32, (wide, 2 * wide), 0)
    b = lax.broadcasted_iota(jnp.int32, (wide, 2 * wide), 1)
    duo = a // (2 * LOW)
    pair = (duo // share * 2 + a // HIGH % 2) * share + duo % share
    value = a // (2 * HIGH) % (LOW // HIGH) * HIGH + a % HIGH
    target = b % wide
    keep = (pair == target // LOW) & ((b >= wide) | (value <= target % LOW))
    pieces = []
    rest = here
    for _ in range(3):
        piece = rest.astype(bf16)
        pieces.append(piece)
        rest = rest - piece.astype(f32)
    spread = lax.dot_general(
        jnp.concatenate(pieces, axis=0), keep.astype(f32).astype(bf16), (((1,), (0,)), ((), ())),
        preferred_element_type=f32,
    )
    spread = spread[:count] + spread[count : 2 * count] + spread[2 * count :]
    level = lax.broadcasted_iota(jnp.int32, (HIGH, wide), 0)

    def running(top):
        inside = spread[top : top + HIGH, :wide]
        upto = spread[top : top + HIGH, wide:]
        for shift in (1, 2, 4):
            upto = upto + jnp.where(level >= shift, pltpu.roll(upto, shift, 0), 0.0)
        before = jnp.where(level >= 1, pltpu.roll(upto, 1, 0), 0.0)
        return inside + before, upto[HIGH - 1 :]

    row_at = lax.broadcasted_iota(jnp.int32, (HIGH, BINS), 0)
    block_at = lax.broadcasted_iota(jnp.int32, (HIGH, BINS), 1) // LOW
    for g in range(groups_each):
        gl, ga = running(g * 2 * HIGH)
        hl, ha = running(g * 2 * HIGH + HIGH)
        gains = (
            gl * gl / (hl + reg_lambda)
            + (ga - gl) * (ga - gl) / (ha - hl + reg_lambda)
            - ga * ga / (ha + reg_lambda)
        )
        if wide < BINS:
            gains = jnp.concatenate([gains, jnp.zeros((HIGH, BINS - wide), f32)], axis=1)
        turned = gains
        for d in range(1, HIGH):
            moved = pltpu.roll(pltpu.roll(gains, HIGH - d, 0), LOW * d, 1)
            turned = jnp.where((row_at + d) % HIGH == block_at, moved, turned)
        each = 2 * duos // share
        for k in range(each):
            gains_ref[g * each + k] = turned[k * share : (k + 1) * share]


def local(n_cls, n_row, binned, labels, logits, elected, split_slot, split_bin):
    rows, classes = logits.shape
    columns = binned.shape[1]
    features = elected.shape[1]
    pairs = classes * features
    share = classes // n_row
    duos = math.gcd(share * features // 2, 4)
    groups_each = share * features // 2 // duos
    unroll = math.gcd(groups_each, UNROLL)
    chips = n_row // 2
    blocks = rows // math.gcd(rows, BLOCK)
    tiles = rows // LANES
    dma = pltpu.SemaphoreType.DMA
    part = (chips, groups_each, 2 * HIGH, duos * 2 * LOW)
    anywhere = pl.BlockSpec(memory_space=pltpu.HBM)
    vmem = pltpu.VMEM

    new, gains = pl.pallas_call(
        functools.partial(kernel, n_cls, n_row, duos, groups_each, unroll, share),
        out_shape=[jax.ShapeDtypeStruct((classes, rows), f32), jax.ShapeDtypeStruct((features, share, BINS), f32)],
        in_specs=[anywhere] * 6,
        out_specs=[pl.BlockSpec(memory_space=pltpu.VMEM)] * 2,
        scratch_shapes=[
            vmem((rows, columns), jnp.int32), vmem((classes, rows), f32), vmem((1, rows), jnp.int32),
            vmem((features, classes), jnp.int32), vmem((1, classes), jnp.int32), vmem((1, classes), jnp.int32),
            vmem((128, 128), f32),
            vmem((pairs + classes, columns), bf16),
            vmem((tiles, pairs, LANES), f32), vmem((tiles, pairs, LANES), f32),
            vmem((classes, rows), f32),
            vmem((tiles, classes, LANES), f32), vmem((tiles, classes, LANES), f32),
            vmem((classes, tiles, 16, LANES), bf16), vmem((classes, tiles, 16, LANES), bf16),
            vmem((n_cls, 2, rows), f32),
            vmem((n_row, classes, LANES), f32),
            vmem(part, f32), vmem(part, f32), vmem(part, f32), vmem(part, f32),
            dma((blocks + 5,)), dma((n_cls,)), dma((n_cls,)), dma((n_row,)), dma((n_row,)),
            dma((chips,)), dma((chips,)), dma((chips,)), dma((chips,)),
        ],
        compiler_params=pltpu.CompilerParams(
            vmem_limit_bytes=52 * 1024 * 1024, collective_id=0, has_side_effects=True,
        ),
        name="round",
    )(
        *[pltpu.with_memory_space_constraint(array, pltpu.HBM) for array in (
            binned, logits.T, labels.reshape(1, rows), elected.T,
            split_slot.reshape(1, classes), split_bin.reshape(1, classes),
        )]
    )
    return new.T, gains.transpose(1, 0, 2)


def solution(mesh):
    return jax.shard_map(
        functools.partial(local, mesh.shape["cls"], mesh.shape["row"]),
        mesh=mesh,
        in_specs=(P("row", None), P("row"), P("row", "cls"), P("cls", None), P("cls"), P("cls")),
        out_specs=(P("row", "cls"), P(("cls", "row"), None, None)),
        check_vma=False,
    )
```

time: 59.8 us -> 34.4 us (0.58)
  Pallas kernels: 55.2 us -> 32.1 us
  local copies, waits for them, and re-layouts: 3.57 us -> 1.42 us
    pallas_call x1, Pallas kernels: 55.2 us -> 32.1 us  [local(): pl.pallas_call(functools.partial(kernel, n_cls, n_row, duos, groups_each,...]
    unnamed x2, local copies, waits for them, and re-layouts: 2.52 us -> 1.42 us
    reshape x3 -> x0, local copies, waits for them, and re-layouts: 1.04 us -> none  [the longest x2 0.93 us: local(): gains = gains.reshape(groups_each, HIGH, group, LOW).transpose(0, 2, 1, 3)]
where the time goes in v1:
time: 34.4 us; the launch traced here: 34.2 us
  Pallas kernels  32.1 us (93%)
  local copies, waits for them, and re-layouts  1.42 us (4%)
  between operations  0.64 us (2%)
    pallas_call x1, Pallas kernels, local(): pl.pallas_call(functools.partial(kernel, n_cls, n_row, duos, groups_each,...  32.1 us
    unnamed x2, local copies, waits for them, and re-layouts  1.42 us

profile of v1, /device:TPU:0, one launch (start us, length us, event | category | flops | bytes accessed | tf_op | source)
XLA Modules:
  0.0 34.2 jit_solution(7708424012034579028)
XLA Ops:
  0.6 32.1 %round.1 = (f32[32,4096]{1,0:T(8,128)S(1)}, f32[12,4,256]{2,1,0:T(4,128)S(1)}) custom-call(s32[4096,512]{1,0:T(8,128)} %binned_hbm.1, f32[32,4096]{1,0:T(8,128)} %bitcast.9, s32[1,4096]{1,0:T(1,128)} %bitcast.10, s32[12,32]{1,0:T(8,128)} %bitcast.11, s32[1,32]{1,0:T(1,128)} %bitcast.12, s32[1,32]{1,0:T(1,128)} %bitcast.13), custom_call_target="tpu_custom_call" | custom-call | tf_op jit(solution)/shard_map/round/pallas_call | solution.py:354
  32.8 0.8 %copy.10 = f32[4096,32]{0,1:T(8,128)} copy(f32[4096,32]{0,1:T(8,128)S(1)} %bitcast.7) | data formatting | bytes 1048576
  33.6 0.6 %copy.11 = f32[4,12,256]{2,0,1:T(4,128)} copy(f32[4,12,256]{2,0,1:T(4,128)S(1)} %bitcast.8) | data formatting | bytes 98304

commit v2 on v1

--- a/solution.py
+++ b/solution.py
@@ -24,14 +24,13 @@
 narrow = jnp.float8_e4m3fn
 
 
-def kernel(
-    n_cls, n_row, duos, groups_each, unroll, share,
+def prepare(
+    n_cls,
     binned_hbm, x_hbm, labels_hbm, elected_hbm, slot_hbm, split_hbm,
-    new_ref, gains_ref,
+    low, high, left, grad_rows, hess_rows, sums_ref,
     binned_ref, x_ref, labels_ref, elected_ref, slot_ref, split_ref,
-    meta, picker, low, high, left, grad_ref, hess_ref, grad_rows, hess_rows, stats, sums,
-    theirs, mine, first, second,
-    load_sem, send_stat, recv_stat, send_sum, recv_sum, send_one, recv_one, send_two, recv_two,
+    meta, picker, grad_ref, hess_ref, stats,
+    load_sem, send_stat, recv_stat,
 ):
     classes, rows = x_ref.shape
     features = elected_ref.shape[0]
@@ -42,33 +41,12 @@
     per_block = block // LANES
     cls = lax.axis_index("cls")
     me = lax.axis_index("row")
-    core = lax.rem(me, 2)
-    chip = me // 2
-    chips = n_row // 2
     barrier = pltpu.get_barrier_semaphore()
 
     def stat_copy(k):
         return pltpu.make_async_remote_copy(
             src_ref=stats.at[0], dst_ref=stats.at[k], send_sem=send_stat.at[k], recv_sem=recv_stat.at[k],
             device_id=(lax.rem(cls + k, n_cls), me), device_id_type=MESH,
-        )
-
-    def sum_copy(k):
-        return pltpu.make_async_remote_copy(
-            src_ref=sums.at[0], dst_ref=sums.at[k], send_sem=send_sum.at[k], recv_sem=recv_sum.at[k],
-            device_id=(cls, lax.rem(me + k, n_row)), device_id_type=MESH,
-        )
-
-    def one_copy(s):
-        return pltpu.make_async_remote_copy(
-            src_ref=theirs.at[s], dst_ref=first.at[s], send_sem=send_one.at[s], recv_sem=recv_one.at[s],
-            device_id=(cls, 2 * chip + 1 - core), device_id_type=MESH,
-        )
-
-    def two_copy(s):
-        return pltpu.make_async_remote_copy(
-            src_ref=mine.at[s], dst_ref=second.at[s], send_sem=send_two.at[s], recv_sem=recv_two.at[s],
-            device_id=(cls, 2 * lax.rem(chip + s + 1, chips) + core), device_id_type=MESH,
         )
 
     small = [
@@ -87,8 +65,6 @@
 
     for k in range(1, n_cls):
         pl.semaphore_signal(barrier, inc=1, device_id=(lax.rem(cls + k, n_cls), me), device_id_type=MESH)
-    for k in range(1, n_row):
-        pl.semaphore_signal(barrier, inc=1, device_id=(cls, lax.rem(me + k, n_row)), device_id_type=MESH)
     for copy in small[:4]:
         copy.start()
     for copy in part:
@@ -132,13 +108,11 @@
             high[b * per_block + j] = top[:, j * LANES : (j + 1) * LANES]
         left[:, b * block : (b + 1) * block] = (picked[pairs:] <= split_column).astype(f32)
 
-    for b in range(blocks // 2):
-        pick(b)
     with jax.named_scope("barrier"):
-        pl.semaphore_wait(barrier, n_cls - 1 + n_row - 1)
+        pl.semaphore_wait(barrier, n_cls - 1)
     for k in range(1, n_cls):
         stat_copy(k).start()
-    for b in range(blocks // 2, blocks):
+    for b in range(blocks):
         pick(b)
 
     small[4].wait()
@@ -171,9 +145,7 @@
     packed = jnp.zeros((classes, LANES), f32)
     for n in range(4):
         packed = jnp.where(spot == n, jnp.sum(totals[n], axis=1, keepdims=True), packed)
-    sums[0] = packed
-    for k in range(1, n_row):
-        sum_copy(k).start()
+    sums_ref[...] = packed
 
     def repeat(c, carry):
         for t in range(tiles):
@@ -185,6 +157,48 @@
 
     with jax.named_scope("repeat"):
         lax.fori_loop(0, classes, repeat, 0)
+
+
+def reduce(
+    n_row, duos, groups_each, unroll, share, features,
+    x_hbm, low, high, left, grad_rows, hess_rows, sums_ref,
+    new_ref, gains_ref,
+    x_ref, sums, work, first, second,
+    load_sem, send_sum, recv_sum, send_one, recv_one, send_two, recv_two,
+):
+    classes, rows = x_ref.shape
+    block = math.gcd(rows, BLOCK)
+    blocks = rows // block
+    cls = lax.axis_index("cls")
+    me = lax.axis_index("row")
+    core = lax.rem(me, 2)
+    chip = me // 2
+    chips = n_row // 2
+    barrier = pltpu.get_barrier_semaphore()
+
+    def sum_copy(k):
+        return pltpu.make_async_remote_copy(
+            src_ref=sums.at[0], dst_ref=sums.at[k], send_sem=send_sum.at[k], recv_sem=recv_sum.at[k],
+            device_id=(cls, lax.rem(me + k, n_row)), device_id_type=MESH,
+        )
+
+    def one_copy(s):
+        return pltpu.make_async_remote_copy(
+            src_ref=work.at[2 * s], dst_ref=first.at[s], send_sem=send_one.at[s], recv_sem=recv_one.at[s],
+            device_id=(cls, 2 * chip + 1 - core), device_id_type=MESH,
+        )
+
+    def two_copy(s):
+        return pltpu.make_async_remote_copy(
+            src_ref=work.at[2 * s + 1], dst_ref=second.at[s], send_sem=send_two.at[s], recv_sem=recv_two.at[s],
+            device_id=(cls, 2 * lax.rem(chip + s + 1, chips) + core), device_id_type=MESH,
+        )
+
+    for k in range(1, n_row):
+        pl.semaphore_signal(barrier, inc=1, device_id=(cls, lax.rem(me + k, n_row)), device_id_type=MESH)
+    load = pltpu.make_async_copy(x_hbm, x_ref, load_sem.at[0])
+    load.start()
+    sums[0] = sums_ref[...]
 
     sub = lax.broadcasted_iota(jnp.int32, (16, LANES), 0) & (HIGH - 1)
     ids = [(sub + HIGH * n).astype(f32).astype(bf16) for n in range(LOW // HIGH)]
@@ -201,11 +215,10 @@
             tops = []
             lows = []
             for d in range(duos):
-                q = g * duos + d
-                c = dest * share + q % share
-                p = q // share * 2 * classes + c
+                c = dest * share + d % share
+                p = g * (duos // share * 2 * classes) + dest * share + (d // share * 2 * classes + d % share)
                 top = [[], []]
-                low_rows = [[] for _ in range(LOW // 16)]
+                hot = [[] for _ in ids]
                 for t in range(step * depth // LANES, (step + 1) * depth // LANES):
 
                     def both(ref):
@@ -214,14 +227,19 @@
                         return jnp.concatenate([a, b], axis=0).astype(bf16)
 
                     lo = both(low)
-                    hot = [jnp.where(lo == i, one, zero) for i in ids]
-                    for n in range(LOW // 16):
-                        low_rows[n].append(jnp.concatenate(hot[2 * n : 2 * n + 2], axis=0).astype(narrow))
-                    same = both(high) == ids[0]
-                    top[0].append(jnp.where(same, grad_rows[c, t], zero))
-                    top[1].append(jnp.where(same, hess_rows[c, t], zero))
+                    hi = both(high)
+                    g_row = grad_rows[c, t]
+                    h_row = hess_rows[c, t]
+                    for n, i in enumerate(ids):
+                        hot[n].append(jnp.where(lo == i, one, zero))
+                    same = hi == ids[0]
+                    top[0].append(jnp.where(same, g_row, zero))
+                    top[1].append(jnp.where(same, h_row, zero))
+                for n in range(0, len(ids), 2):
+                    lows.append(jnp.concatenate([
+                        jnp.concatenate(pair, axis=0).astype(narrow) for pair in zip(hot[n], hot[n + 1])
+                    ], axis=1))
                 tops += [jnp.concatenate(r, axis=1) for r in top]
-                lows += [jnp.concatenate(r, axis=1) for r in low_rows]
             product = lax.dot_general(
                 jnp.concatenate(tops, axis=0), jnp.concatenate(lows, axis=0), NT, preferred_element_type=f32
             )
@@ -234,32 +252,51 @@
                 kept = piece if kept is None else jnp.where(lane_pair == 2 * d + s, piece, kept)
         return kept
 
-    def fill(target_ref, s, dest):
-        def some(i, carry):
+    def each_dest(j, carry):
+        def some(i, inner):
             for u in range(unroll):
-                target_ref[s, i * unroll + u] = one_group(dest, i * unroll + u)
-            return carry
+                at = (j * groups_each) + i * unroll + u
+                k = at // groups_each
+                dest = 2 * lax.rem(chip + k // 2 + 1, chips) + lax.rem(core + 1 + lax.rem(k, 2), 2)
+                g = lax.rem(at, groups_each)
+                work[k, g] = one_group(dest, g)
+            return inner
 
         lax.fori_loop(0, groups_each // unroll, some, 0)
-
-    def each_chip(s, carry):
-        dest = lax.rem(chip + s + 1, chips)
-        fill(theirs, s, 2 * dest + 1 - core)
-        one_copy(s).start()
-        fill(mine, s, 2 * dest + core)
-
-        @pl.when(s < chips - 1)
+        s = j // 2
+        own = lax.rem(j, 2)
+
+        def pass_on(n):
+            one_copy(n).wait_recv()
+            work[2 * n + 1] = work[2 * n + 1] + first[n]
+            two_copy(n).start()
+
+        @pl.when(j == 1)
         def _():
-            with jax.named_scope("onewait"):
-                one_copy(s).wait_recv()
-            mine[s] = mine[s] + first[s]
-            two_copy(s).start()
+            with jax.named_scope("rowbarrier"):
+                pl.semaphore_wait(barrier, n_row - 1)
+            for k in range(1, n_row):
+                sum_copy(k).start()
+            one_copy(0).start()
+
+        @pl.when((own == 0) & (j > 1))
+        def _():
+            one_copy(s).start()
+
+        @pl.when(j == 3)
+        def _():
+            pass_on(0)
+
+        @pl.when((own == 1) & (s > 0) & (s < chips - 1))
+        def _():
+            pass_on(s)
 
         return carry
 
     with jax.named_scope("hist"):
-        lax.fori_loop(0, chips, each_chip, 0)
-
+        lax.fori_loop(0, 2 * chips, each_dest, 0)
+
+    load.wait()
     total = sums[0]
     with jax.named_scope("sumwait"):
         for k in range(1, n_row):
@@ -280,7 +317,7 @@
             one_copy(s).wait_send()
         for s in range(chips - 1):
             two_copy(s).wait()
-    summed = mine[chips - 1] + first[chips - 1]
+    summed = work[2 * chips - 1] + first[chips - 1]
     for s in range(chips - 1):
         summed = summed + second[s]
     count = groups_each * 2 * HIGH
@@ -334,6 +371,17 @@
             gains_ref[g * each + k] = turned[k * share : (k + 1) * share]
 
 
+def deliver(new_ref, gains_ref, new_hbm, gains_hbm, sem):
+    copies = [
+        pltpu.make_async_copy(new_ref, new_hbm, sem.at[0]),
+        pltpu.make_async_copy(gains_ref, gains_hbm, sem.at[1]),
+    ]
+    for copy in copies:
+        copy.start()
+    for copy in copies:
+        copy.wait()
+
+
 def local(n_cls, n_row, binned, labels, logits, elected, split_slot, split_bin):
     rows, classes = logits.shape
     columns = binned.shape[1]
@@ -351,36 +399,64 @@
     anywhere = pl.BlockSpec(memory_space=pltpu.HBM)
     vmem = pltpu.VMEM
 
-    new, gains = pl.pallas_call(
-        functools.partial(kernel, n_cls, n_row, duos, groups_each, unroll, share),
-        out_shape=[jax.ShapeDtypeStruct((classes, rows), f32), jax.ShapeDtypeStruct((features, share, BINS), f32)],
+    inside = pl.BlockSpec(memory_space=pltpu.VMEM)
+    logits_t = pltpu.with_memory_space_constraint(logits.T, pltpu.HBM)
+    made = pl.pallas_call(
+        functools.partial(prepare, n_cls),
+        out_shape=[
+            jax.ShapeDtypeStruct((tiles, pairs, LANES), f32), jax.ShapeDtypeStruct((tiles, pairs, LANES), f32),
+            jax.ShapeDtypeStruct((classes, rows), f32),
+            jax.ShapeDtypeStruct((classes, tiles, 16, LANES), bf16),
+            jax.ShapeDtypeStruct((classes, tiles, 16, LANES), bf16),
+            jax.ShapeDtypeStruct((classes, LANES), f32),
+        ],
         in_specs=[anywhere] * 6,
-        out_specs=[pl.BlockSpec(memory_space=pltpu.VMEM)] * 2,
+        out_specs=[inside] * 6,
         scratch_shapes=[
             vmem((rows, columns), jnp.int32), vmem((classes, rows), f32), vmem((1, rows), jnp.int32),
             vmem((features, classes), jnp.int32), vmem((1, classes), jnp.int32), vmem((1, classes), jnp.int32),
             vmem((128, 128), f32),
             vmem((pairs + classes, columns), bf16),
-            vmem((tiles, pairs, LANES), f32), vmem((tiles, pairs, LANES), f32),
-            vmem((classes, rows), f32),
             vmem((tiles, classes, LANES), f32), vmem((tiles, classes, LANES), f32),
-            vmem((classes, tiles, 16, LANES), bf16), vmem((classes, tiles, 16, LANES), bf16),
             vmem((n_cls, 2, rows), f32),
-            vmem((n_row, classes, LANES), f32),
-            vmem(part, f32), vmem(part, f32), vmem(part, f32), vmem(part, f32),
-            dma((blocks + 5,)), dma((n_cls,)), dma((n_cls,)), dma((n_row,)), dma((n_row,)),
+            dma((blocks + 5,)), dma((n_cls,)), dma((n_cls,)),
+        ],
+        compiler_params=pltpu.CompilerParams(
+            vmem_limit_bytes=24 * 1024 * 1024, collective_id=0, has_side_effects=True,
+        ),
+        name="prepare",
+    )(
+        pltpu.with_memory_space_constraint(binned, pltpu.HBM), logits_t,
+        *[pltpu.with_memory_space_constraint(array, pltpu.HBM) for array in (
+            labels.reshape(1, rows), elected.T, split_slot.reshape(1, classes), split_bin.reshape(1, classes),
+        )]
+    )
+    new, gains = pl.pallas_call(
+        functools.partial(reduce, n_row, duos, groups_each, unroll, share, features),
+        out_shape=[
+            jax.ShapeDtypeStruct((classes, rows), f32), jax.ShapeDtypeStruct((features, share, BINS), f32),
+        ],
+        in_specs=[anywhere] + [inside] * 6,
+        out_specs=[inside] * 2,
+        scratch_shapes=[
+            vmem((classes, rows), f32), vmem((n_row, classes, LANES), f32),
+            vmem((2 * chips, *part[1:]), f32), vmem(part, f32), vmem(part, f32),
+            dma((1,)), dma((n_row,)), dma((n_row,)),
             dma((chips,)), dma((chips,)), dma((chips,)), dma((chips,)),
         ],
         compiler_params=pltpu.CompilerParams(
-            vmem_limit_bytes=52 * 1024 * 1024, collective_id=0, has_side_effects=True,
+            vmem_limit_bytes=24 * 1024 * 1024, collective_id=1, has_side_effects=True,
         ),
-        name="round",
-    )(
-        *[pltpu.with_memory_space_constraint(array, pltpu.HBM) for array in (
-            binned, logits.T, labels.reshape(1, rows), elected.T,
-            split_slot.reshape(1, classes), split_bin.reshape(1, classes),
-        )]
-    )
+        name="reduce",
+    )(logits_t, *[pltpu.with_memory_space_constraint(array, pltpu.VMEM) for array in made])
+    new, gains = pl.pallas_call(
+        deliver,
+        out_shape=[jax.ShapeDtypeStruct(new.shape, f32), jax.ShapeDtypeStruct(gains.shape, f32)],
+        in_specs=[inside] * 2,
+        out_specs=[pl.BlockSpec(memory_space=pltpu.HBM)] * 2,
+        scratch_shapes=[dma((2,))],
+        name="deliver",
+    )(*[pltpu.with_memory_space_constraint(array, pltpu.VMEM) for array in (new, gains)])
     return new.T, gains.transpose(1, 0, 2)
 
 

time: 34.4 us -> 30.2 us (0.88)
  Pallas kernels: 32.1 us -> 29.4 us
  local copies, waits for them, and re-layouts: 1.42 us -> 0 us
    pallas_call x1 -> x3, Pallas kernels: 32.1 us -> 29.4 us  [the longest x1 19.3 us: local(): pl.pallas_call(functools.partial(reduce, n_row, duos, groups_each, unroll...]
    unnamed x2 -> x0, local copies, waits for them, and re-layouts: 1.42 us -> none
where the time goes in v2:
time: 30.2 us; the launch traced here: 30 us
  Pallas kernels  29.4 us (97%)
  between operations  0.65 us (2%)
    pallas_call x1, Pallas kernels, local(): pl.pallas_call(functools.partial(reduce, n_row, duos, groups_each, unroll...  19.3 us
    pallas_call x1, Pallas kernels, local(): pl.pallas_call(functools.partial(prepare, n_cls), out_shape=[jax.ShapeDty...  9.24 us
    pallas_call x1, Pallas kernels, local(): pl.pallas_call(deliver, out_shape=[jax.ShapeDtypeStruct(new.shape, f32),...  0.81 us

profile of v2, /device:TPU:0, one launch (start us, length us, event | category | flops | bytes accessed | tf_op | source)
XLA Modules:
  0.0 30.0 jit_solution(11865339752916382084)
XLA Ops:
  0.6 9.2 %prepare.1 = (f32[32,384,128]{2,1,0:T(8,128)S(1)}, f32[32,384,128]{2,1,0:T(8,128)S(1)}, f32[32,4096]{1,0:T(8,128)S(1)}, bf16[32,32,16,128]{3,2,1,0:T(8,128)(2,1)...) custom-call(s32[4096,512]{1,0:T(8,128)} %binned_hbm.1, f32[32,4096]{1,0:T(8,128)} %bitcast.7, ...), custom_call_target="tpu_custom_call" | custom-call | tf_op jit(solution)/shard_map/prepare/pallas_call | solution.py:404
  9.9 19.3 %reduce.1 = (f32[32,4096]{1,0:T(8,128)S(1)}, f32[12,4,256]{2,1,0:T(4,128)S(1)}) custom-call(f32[32,4096]{1,0:T(8,128)} %bitcast.8, f32[32,384,128]{2,1,0:T(8,128)S(1)} %get-tuple-element.12.low, f32[32,384,128]{2,1,0:T(8,128)S(1)} %get-tuple-element.13.high, f32[32,4096]{1,0:T(8,128)S(1)} %get-tuple-element.14.left, ...), custom_call_target="tpu_custom_call" | custom-call | tf_op jit(solution)/shard_map/reduce/pallas_call | solution.py:434
  29.2 0.8 %deliver.1 = (f32[32,4096]{1,0:T(8,128)}, f32[12,4,256]{2,1,0:T(4,128)}) custom-call(f32[32,4096]{1,0:T(8,128)S(1)} %get-tuple-element.18.new_ref, f32[12,4,256]{2,1,0:T(4,128)S(1)} %get-tuple-element.19.gains_ref), custom_call_target="tpu_custom_call" | custom-call | tf_op jit(solution)/shard_map/deliver/pallas_call | solution.py:452

commit v3 on v2

--- a/solution.py
+++ b/solution.py
@@ -43,9 +43,13 @@
     me = lax.axis_index("row")
     barrier = pltpu.get_barrier_semaphore()
 
-    def stat_copy(k):
+    halves = stats.shape[0]
+    per_half = blocks // halves
+
+    def stat_copy(h, k):
         return pltpu.make_async_remote_copy(
-            src_ref=stats.at[0], dst_ref=stats.at[k], send_sem=send_stat.at[k], recv_sem=recv_stat.at[k],
+            src_ref=stats.at[h, 0], dst_ref=stats.at[h, k],
+            send_sem=send_stat.at[h, k], recv_sem=recv_stat.at[h, k],
             device_id=(lax.rem(cls + k, n_cls), me), device_id_type=MESH,
         )
 
@@ -93,8 +97,9 @@
         cols = slice(b * block, (b + 1) * block)
         x = x_ref[:, cols]
         local_max = jnp.max(x, axis=0, keepdims=True)
-        stats[0, 0:1, cols] = local_max
-        stats[0, 1:2, cols] = jnp.sum(jnp.exp(x - local_max), axis=0, keepdims=True)
+        half = slice(b % per_half * block, (b % per_half + 1) * block)
+        stats[b // per_half, 0, 0:1, half] = local_max
+        stats[b // per_half, 0, 1:2, half] = jnp.sum(jnp.exp(x - local_max), axis=0, keepdims=True)
 
     def pick(b):
         part[b].wait()
@@ -110,26 +115,29 @@
 
     with jax.named_scope("barrier"):
         pl.semaphore_wait(barrier, n_cls - 1)
-    for k in range(1, n_cls):
-        stat_copy(k).start()
+    for h in range(halves):
+        for k in range(1, n_cls):
+            stat_copy(h, k).start()
     for b in range(blocks):
         pick(b)
 
     small[4].wait()
-    with jax.named_scope("statwait"):
-        for k in range(1, n_cls):
-            stat_copy(k).wait()
     class_ids = cls * classes + lax.broadcasted_iota(jnp.int32, (classes, block), 0)
     totals = [jnp.zeros((classes, LANES), f32) for _ in range(4)]
     for b in range(blocks):
         cols = slice(b * block, (b + 1) * block)
-        local_max = stats[0, 0:1, cols]
+        h = b // per_half
+        if b % per_half == 0:
+            for k in range(1, n_cls):
+                stat_copy(h, k).wait()
+        half = slice(b % per_half * block, (b % per_half + 1) * block)
+        local_max = stats[h, 0, 0:1, half]
         highest = local_max
         for k in range(1, n_cls):
-            highest = jnp.maximum(highest, stats[k, 0:1, cols])
-        denom = stats[0, 1:2, cols] * jnp.exp(local_max - highest)
+            highest = jnp.maximum(highest, stats[h, k, 0:1, half])
+        denom = stats[h, 0, 1:2, half] * jnp.exp(local_max - highest)
         for k in range(1, n_cls):
-            denom = denom + stats[k, 1:2, cols] * jnp.exp(stats[k, 0:1, cols] - highest)
+            denom = denom + stats[h, k, 1:2, half] * jnp.exp(stats[h, k, 0:1, half] - highest)
         probs = jnp.exp(x_ref[:, cols] - highest) / denom
         target = (labels_ref[:, cols] == class_ids).astype(f32)
         grad = (probs - target).astype(bf16).astype(f32)
@@ -393,6 +401,7 @@
     unroll = math.gcd(groups_each, UNROLL)
     chips = n_row // 2
     blocks = rows // math.gcd(rows, BLOCK)
+    halves = math.gcd(blocks, 2)
     tiles = rows // LANES
     dma = pltpu.SemaphoreType.DMA
     part = (chips, groups_each, 2 * HIGH, duos * 2 * LOW)
@@ -418,8 +427,8 @@
             vmem((128, 128), f32),
             vmem((pairs + classes, columns), bf16),
             vmem((tiles, classes, LANES), f32), vmem((tiles, classes, LANES), f32),
-            vmem((n_cls, 2, rows), f32),
-            dma((blocks + 5,)), dma((n_cls,)), dma((n_cls,)),
+            vmem((halves, n_cls, 2, rows // halves), f32),
+            dma((blocks + 5,)), dma((halves, n_cls)), dma((halves, n_cls)),
         ],
         compiler_params=pltpu.CompilerParams(
             vmem_limit_bytes=24 * 1024 * 1024, collective_id=0, has_side_effects=True,

time: 30.2 us -> 30.2 us (level)
  no operation moved by 1% of the time
where the time goes in v3:
time: 30.2 us; the launch traced here: 30 us
  Pallas kernels  29.4 us (97%)
  between operations  0.65 us (2%)
    pallas_call x1, Pallas kernels, local(): pl.pallas_call(functools.partial(reduce, n_row, duos, groups_each, unroll...  19.3 us
    pallas_call x1, Pallas kernels, local(): pl.pallas_call(functools.partial(prepare, n_cls), out_shape=[jax.ShapeDty...  9.28 us
    pallas_call x1, Pallas kernels, local(): pl.pallas_call(deliver, out_shape=[jax.ShapeDtypeStruct(new.shape, f32),...  0.81 us

profile of v3, /device:TPU:0, one launch (start us, length us, event | category | flops | bytes accessed | tf_op | source)
XLA Modules:
  0.0 30.0 jit_solution(1660772801012839768)
XLA Ops:
  0.6 9.3 %prepare.1 = (f32[32,384,128]{2,1,0:T(8,128)S(1)}, f32[32,384,128]{2,1,0:T(8,128)S(1)}, f32[32,4096]{1,0:T(8,128)S(1)}, bf16[32,32,16,128]{3,2,1,0:T(8,128)(2,1)...) custom-call(s32[4096,512]{1,0:T(8,128)} %binned_hbm.1, f32[32,4096]{1,0:T(8,128)} %bitcast.7, ...), custom_call_target="tpu_custom_call" | custom-call | tf_op jit(solution)/shard_map/prepare/pallas_call | solution.py:413
  9.9 19.3 %reduce.1 = (f32[32,4096]{1,0:T(8,128)S(1)}, f32[12,4,256]{2,1,0:T(4,128)S(1)}) custom-call(f32[32,4096]{1,0:T(8,128)} %bitcast.8, f32[32,384,128]{2,1,0:T(8,128)S(1)} %get-tuple-element.12.low, f32[32,384,128]{2,1,0:T(8,128)S(1)} %get-tuple-element.13.high, f32[32,4096]{1,0:T(8,128)S(1)} %get-tuple-element.14.left, ...), custom_call_target="tpu_custom_call" | custom-call | tf_op jit(solution)/shard_map/reduce/pallas_call | solution.py:443
  29.2 0.8 %deliver.1 = (f32[32,4096]{1,0:T(8,128)}, f32[12,4,256]{2,1,0:T(4,128)}) custom-call(f32[32,4096]{1,0:T(8,128)S(1)} %get-tuple-element.18.new_ref, f32[12,4,256]{2,1,0:T(4,128)S(1)} %get-tuple-element.19.gains_ref), custom_call_target="tpu_custom_call" | custom-call | tf_op jit(solution)/shard_map/deliver/pallas_call | solution.py:461
